TPU v7x, 64 devices: a 2x2x8 block of a 4x4x8 slice. The times are simulated.
64 devices in a mesh: dp: 4 (over x, y), tp: 16 (over z, core).
Axes of the slice: x: 2, y: 2, z: 8, core: 2. Of those that a mesh axis runs over, the one named last changes fastest.
The devices are a block of a 4x4x8 slice.
Arguments:
- y_one: float32 [64, 256, 1024], P('dp', 'tp'), parts along dimension 0
- y_two: float32 [64, 256, 1024], P('dp', 'tp'), parts along dimension 0
- dy_one: float32 [64, 256, 1024], P('dp', 'tp'), parts along dimension 0
- dy_two: float32 [64, 256, 1024], P('dp', 'tp'), parts along dimension 0
- w_qkv: bfloat16 [1, 1024, 16, 3, 64], P(None, None, 'tp')
- w_out: bfloat16 [1, 16, 64, 1024], P(None, 'tp')
- w_up: bfloat16 [1, 1024, 4096], P(None, None, 'tp')
- w_down: bfloat16 [1, 4096, 1024], P(None, 'tp')
Outputs:
- output 1: float32 [64, 256, 1024], P('dp', 'tp'), parts along dimension 0
- output 2: float32 [64, 256, 1024], P('dp', 'tp'), parts along dimension 0
- output 3: float32 [64, 256, 1024], P('dp', 'tp'), parts along dimension 0
- output 4: float32 [64, 256, 1024], P('dp', 'tp'), parts along dimension 0
- output 5: float32 [4, 1024, 16, 3, 64], P('dp', None, 'tp'), parts along dimension 0
- output 6: float32 [4, 16, 64, 1024], P('dp', 'tp'), parts along dimension 0
- output 7: float32 [4, 1024, 4096], P('dp', None, 'tp'), parts along dimension 0
- output 8: float32 [4, 4096, 1024], P('dp', 'tp'), parts along dimension 0
There are 4 independent parts. A program takes and returns all parts, laid end to end along the dimension named above; an argument that names none is the same for every part.
All inputs are finite; a program needn't handle non-finite values.
Results may differ from a plain program's by a relative error of at most 0.00846033.
Values are sent between devices in bfloat16 or wider.
A program may use at most 768 MiB of HBM per device.

v0:
```python
import jax
import jax.numpy as jnp
from jax import lax
from jax.sharding import PartitionSpec as P

RMS_EPS = 1e-6


def rms_norm(tensor):
    return tensor * lax.rsqrt(jnp.mean(tensor * tensor, axis=-1, keepdims=True) + RMS_EPS)


def rms_back(tensor, grad_in):
    inv_rms = lax.rsqrt(jnp.mean(tensor * tensor, axis=-1, keepdims=True) + RMS_EPS)
    return inv_rms * grad_in - tensor * (inv_rms * inv_rms * inv_rms) * jnp.mean(grad_in * tensor, axis=-1, keepdims=True)


def gelu_tanh(tensor):
    return jax.nn.gelu(tensor, approximate=True)


def gather_positions(tensor):
    return lax.all_gather(tensor, "tp", axis=1, tiled=True)


def scatter_positions(tensor):
    return lax.psum_scatter(tensor, "tp", scatter_dimension=1, tiled=True)


def local_backward(y_one, y_two, dy_one, dy_two, w_qkv, w_out, w_up, w_down):
    n_layers = w_qkv.shape[0]
    attn_scale = w_qkv.shape[4] ** -0.5
    grads_qkv, grads_out, grads_up, grads_down = [], [], [], []
    for layer_idx in reversed(range(n_layers)):
        wq_layer = w_qkv[layer_idx]
        wo_layer = w_out[layer_idx]
        wu_layer = w_up[layer_idx]
        wd_layer = w_down[layer_idx]
        u_mlp = gather_positions(rms_norm(y_one).astype(jnp.bfloat16))
        pre_act = jnp.einsum("bsh,hf->bsf", u_mlp, wu_layer, preferred_element_type=jnp.float32)
        hidden, gelu_pull = jax.vjp(gelu_tanh, pre_act)
        hidden_b = hidden.astype(jnp.bfloat16)
        g_part = jnp.einsum("bsf,fh->bsh", hidden_b, wd_layer, preferred_element_type=jnp.float32)
        x_two = y_two - scatter_positions(g_part)
        cot_mlp = gather_positions(dy_two.astype(jnp.bfloat16))
        grads_down.append(jnp.einsum("bsf,bsh->fh", hidden_b, cot_mlp, preferred_element_type=jnp.float32))
        d_hidden = jnp.einsum("bsh,fh->bsf", cot_mlp, wd_layer, preferred_element_type=jnp.float32)
        d_pre = gelu_pull(d_hidden)[0].astype(jnp.bfloat16)
        grads_up.append(jnp.einsum("bsh,bsf->hf", u_mlp, d_pre, preferred_element_type=jnp.float32))
        du_mlp = jnp.einsum("bsf,hf->bsh", d_pre, wu_layer, preferred_element_type=jnp.float32)
        dy_one = dy_one + rms_back(y_one, scatter_positions(du_mlp))
        u_att = gather_positions(rms_norm(x_two).astype(jnp.bfloat16))
        qkv_all = jnp.einsum("bsh,hnjd->jbnsd", u_att, wq_layer, preferred_element_type=jnp.float32).astype(jnp.bfloat16)
        q_heads, k_heads, v_heads = qkv_all[0], qkv_all[1], qkv_all[2]
        scores = jnp.einsum("bnqd,bnkd->bnqk", q_heads, k_heads, preferred_element_type=jnp.float32) * attn_scale
        attn_prob = jax.nn.softmax(scores, axis=-1)
        prob_b = attn_prob.astype(jnp.bfloat16)
        context = jnp.einsum("bnqk,bnkd->bnqd", prob_b, v_heads, preferred_element_type=jnp.float32).astype(jnp.bfloat16)
        f_part = jnp.einsum("bnqd,ndh->bqh", context, wo_layer, preferred_element_type=jnp.float32)
        x_one = y_one - scatter_positions(f_part)
        cot_att = gather_positions(dy_one.astype(jnp.bfloat16))
        grads_out.append(jnp.einsum("bnqd,bqh->ndh", context, cot_att, preferred_element_type=jnp.float32))
        d_context = jnp.einsum("bqh,ndh->bnqd", cot_att, wo_layer, preferred_element_type=jnp.float32).astype(jnp.bfloat16)
        d_prob = jnp.einsum("bnqd,bnkd->bnqk", d_context, v_heads, preferred_element_type=jnp.float32)
        d_value = jnp.einsum("bnqk,bnqd->bnkd", prob_b, d_context, preferred_element_type=jnp.float32)
        d_scores = (attn_prob * (d_prob - jnp.sum(d_prob * attn_prob, axis=-1, keepdims=True)) * attn_scale).astype(jnp.bfloat16)
        d_query = jnp.einsum("bnqk,bnkd->bnqd", d_scores, k_heads, preferred_element_type=jnp.float32)
        d_key = jnp.einsum("bnqk,bnqd->bnkd", d_scores, q_heads, preferred_element_type=jnp.float32)
        d_qkv = jnp.stack([d_query.astype(jnp.bfloat16), d_key.astype(jnp.bfloat16), d_value.astype(jnp.bfloat16)])
        grads_qkv.append(jnp.einsum("bsh,jbnsd->hnjd", u_att, d_qkv, preferred_element_type=jnp.float32))
        du_att = jnp.einsum("jbnsd,hnjd->bsh", d_qkv, wq_layer, preferred_element_type=jnp.float32)
        dx_two = dy_two + rms_back(x_two, scatter_positions(du_att))
        y_one, y_two, dy_two = x_one, x_two, dx_two
    return (y_one, y_two, dy_one, dy_two, jnp.stack(grads_qkv[::-1]), jnp.stack(grads_out[::-1]), jnp.stack(grads_up[::-1]), jnp.stack(grads_down[::-1]))


def solution(mesh):
    state_spec = P("dp", "tp", None)
    in_specs = (state_spec, state_spec, state_spec, state_spec, P(None, None, "tp", None, None), P(None, "tp", None, None), P(None, None, "tp"), P(None, "tp", None))
    out_specs = (state_spec, state_spec, state_spec, state_spec, P("dp", None, "tp", None, None), P("dp", "tp", None, None), P("dp", None, "tp"), P("dp", "tp", None))
    return jax.shard_map(local_backward, mesh=mesh, in_specs=in_specs, out_specs=out_specs, check_vma=False)
```

profile of v0, /device:TPU:21, one launch (start us, length us, event | category | flops | bytes accessed | tf_op | source)
XLA Modules:
  0.0 682.5 jit_solution(7982590105724018326)
XLA Ops:
  7.2 0.0 copy-start
  7.2 0.1 all-gather.5.cloned.1.call-start
  7.3 1.4 multiply_reduce_fusion.5
  8.7 0.6 multiply_multiply_fusion.3
  9.3 2.1 multiply_convert_fusion.3
  11.4 0.1 all-gather.5.cloned.1.call-update
  11.5 0.1 reduce-scatter.5.cloned.1.call-start
  11.6 57.6 %all-gather.5.cloned.1.call-done = bf16[16,256,1024]{2,1,0:T(8,128)(2,1)} async-done(((bf16[16,16,1024]{2,1,0:T(8,128)(2,1)}), bf16[16,256,1024]{2,1,0:T(8,128)(2,1)}) %all-gather.5.cloned.1.call-update) | async-done | bytes 8388624 | tf_op jit(solution)/shard_map/all_gather | solution.py:23
  69.2 6.0 fusion.57
  75.1 1.9 copy-done.4
  77.1 8.3 %fusion.53 = f32[16,256,1024]{2,1,0:T(8,128)} fusion(bf16[1,256,1024]{2,1,0:T(8,128)(2,1)S(1)} %copy-done, f32[16,256,256]{2,1,0:T(8,128)S(1)} %fusion.57), kind=kOutput, calls=%fused_computation.58 | convolution fusion | flops 2156920832 | bytes 21495808 | tf_op jit(solution)/shard_map/bsf,fh->bsh/dot_general | solution.py:43
  85.4 0.1 reduce-scatter.5.cloned.1.call-update
  85.5 0.1 all-gather.9.cloned.1.call-start
  85.5 1.1 copy-done.8
  86.6 0.9 convert_element_type.69
  87.5 0.1 all-gather.9.cloned.1.call-update
  87.6 0.1 all-gather.7.cloned.1.call-start
  87.6 92.8 %reduce-scatter.5.cloned.1.call-done = f32[16,16,1024]{2,1,0:T(8,128)} async-done(((f32[16,256,1024]{2,1,0:T(8,128)}), f32[16,16,1024]{2,1,0:T(8,128)}) %reduce-scatter.5.cloned.1.call-update) | async-done | bytes 1048592 | tf_op jit(solution)/shard_map/reduce_scatter | solution.py:27
  180.4 1.4 multiply_reduce_fusion.4
  181.9 0.7 multiply_multiply_fusion.2
  182.6 0.3 copy-done.2
  182.8 0.9 multiply_convert_fusion.2
  183.8 0.1 all-gather.7.cloned.1.call-update
  183.8 0.0 copy-start.12
  183.8 0.1 reduce-scatter.9.cloned.1.call-start
  183.9 51.0 %all-gather.9.cloned.1.call-done = bf16[16,256,1024]{2,1,0:T(8,128)(2,1)} async-done(((bf16[16,16,1024]{2,1,0:T(8,128)(2,1)}), bf16[16,256,1024]{2,1,0:T(8,128)(2,1)}) %all-gather.9.cloned.1.call-update) | async-done | bytes 8388624 | tf_op jit(solution)/shard_map/all_gather | solution.py:23
  234.9 10.0 %fusion.12 = bf16[16,256,256]{2,1,0:T(8,128)(2,1)S(1)} fusion(f32[16,256,256]{2,1,0:T(8,128)} %copy-done.4, bf16[16,256,1024]{2,1,0:T(8,128)(2,1)} %all-gather.9.cloned.1.call-done, bf16[1,256,1024]{2,1,0:T(8,128)(2,1)S(1)} %copy-done), kind=kOutput, calls=%fused_computation.15 | convolution fusion | flops 2168455168 | bytes 15204352 | tf_op jit(solution)/shard_map/bsh,fh->bsf/dot_general | solution.py:47
  244.9 8.1 %fusion.55 = f32[16,256,1024]{2,1,0:T(8,128)} fusion(bf16[16,256,256]{2,1,0:T(8,128)(2,1)S(1)} %fusion.12, bf16[1,1024,256]{2,1,0:T(8,128)(2,1)S(1)} %copy-done.12), kind=kOutput, calls=%fused_computation.60 | convolution fusion | flops 2147483648 | bytes 19398656 | tf_op jit(solution)/shard_map/bsf,hf->bsh/dot_general | solution.py:50
  253.0 0.1 reduce-scatter.9.cloned.1.call-update
  253.1 0.2 reduce-scatter.7.cloned.1.call-start
  253.3 34.7 %all-gather.7.cloned.1.call-done = bf16[16,256,1024]{2,1,0:T(8,128)(2,1)} async-done(((bf16[16,16,1024]{2,1,0:T(8,128)(2,1)}), bf16[16,256,1024]{2,1,0:T(8,128)(2,1)}) %all-gather.7.cloned.1.call-update) | async-done | bytes 8388624 | tf_op jit(solution)/shard_map/all_gather | solution.py:23
  288.0 6.3 fusion.31
  294.3 0.7 fusion.60
  295.1 3.1 fusion.74
  298.2 0.0 copy-start.19
  298.2 0.0 copy-start.13
  298.3 0.5 convolution_convert_fusion.1
  298.7 1.4 copy-done.6
  300.2 0.0 copy-done.19
  300.2 8.1 %fusion.64 = f32[16,256,1024]{2,1,0:T(8,128)} fusion(bf16[16,256,64]{1,2,0:T(8,128)(2,1)S(1)} %convolution_convert_fusion.1, bf16[1,1,64,1024]{3,2,1,0:T(8,128)(2,1)S(1)} %copy-done.13), kind=kOutput, calls=%fused_computation.69 | convolution fusion | flops 536870912 | bytes 17432576 | tf_op jit(solution)/shard_map/bnqd,ndh->bqh/dot_general | solution.py:59
  308.3 0.1 reduce-scatter.7.cloned.1.call-update
  308.4 0.1 all-gather.11.cloned.1.call-start
  308.4 76.7 %reduce-scatter.9.cloned.1.call-done = f32[16,16,1024]{2,1,0:T(8,128)} async-done(((f32[16,256,1024]{2,1,0:T(8,128)}), f32[16,16,1024]{2,1,0:T(8,128)}) %reduce-scatter.9.cloned.1.call-update) | async-done | bytes 1048592 | tf_op jit(solution)/shard_map/reduce_scatter | solution.py:27
  385.1 1.7 multiply_reduce_fusion.3
  386.8 96.5 %reduce-scatter.7.cloned.1.call-done = f32[16,16,1024]{2,1,0:T(8,128)} async-done(((f32[16,256,1024]{2,1,0:T(8,128)}), f32[16,16,1024]{2,1,0:T(8,128)}) %reduce-scatter.7.cloned.1.call-update) | async-done | bytes 1048592 | tf_op jit(solution)/shard_map/reduce_scatter | solution.py:27
  483.3 4.0 fusion.73
  487.3 0.1 all-gather.11.cloned.1.call-update
  487.3 0.1 reduce-scatter.11.cloned.1.call-start
  487.4 52.3 %all-gather.11.cloned.1.call-done = bf16[16,256,1024]{2,1,0:T(8,128)(2,1)} async-done(((bf16[16,16,1024]{2,1,0:T(8,128)(2,1)}), bf16[16,256,1024]{2,1,0:T(8,128)(2,1)}) %all-gather.11.cloned.1.call-update) | async-done | bytes 8388624 | tf_op jit(solution)/shard_map/all_gather | solution.py:23
  539.7 6.2 convolution_convert_fusion
  545.9 1.5 fusion.43
  547.4 3.8 fusion.59
  551.1 8.2 %fusion.47 = bf16[1,16,1,256,64]{3,4,1,2,0:T(8,128)(2,1)} fusion(f32[16,256,256]{1,2,0:T(8,128)} %fusion.59, bf16[3,16,1,256,64]{3,4,0,1,2:T(8,128)(2,1)} %copy-done.10, f32[16,256,256]{1,2,0:T(8,128)} %copy-done.6, f32[16,256]{1,0:T(8,128)} %copy-done.19), kind=kOutput, calls=%fused_computation.42 | convolution fusion | flops 141824256 | bytes 17858560 | tf_op jit(solution)/shard_map/bnqk,bnkd->bnqd/dot_general | solution.py:67
  559.3 8.0 %fusion.44 = bf16[1,16,1,256,64]{3,4,1,2,0:T(8,128)(2,1)} fusion(f32[16,256,256]{1,2,0:T(8,128)} %fusion.59, bf16[3,16,1,256,64]{3,4,0,1,2:T(8,128)(2,1)} %copy-done.10, f32[16,256,256]{1,2,0:T(8,128)} %copy-done.6, f32[16,256]{1,0:T(8,128)} %copy-done.19), kind=kOutput, calls=%fused_computation.41 | convolution fusion | flops 141824256 | bytes 17858560 | tf_op jit(solution)/shard_map/bnqk,bnqd->bnkd/dot_general | solution.py:68
  567.3 9.3 %convolution_bitcast_fusion = f32[16,256,1024]{2,1,0:T(8,128)} fusion(bf16[1,16,1,256,64]{3,4,1,2,0:T(8,128)(2,1)S(1)} %fusion.43, bf16[1,16,1,256,64]{3,4,1,2,0:T(8,128)(2,1)} %fusion.44, bf16[1,16,1,256,64]{3,4,1,2,0:T(8,128)(2,1)} %fusion.47, bf16[1,1024,1,3,64]{1,4,3,2,0:T(8,128)(2,1)S(1)} %copy-done.16), kind=kOutput, calls=%fused_computation.2 | convolution fusion | flops 1612185600 | bytes 18743296 | tf_op jit(solution)/shard_map/jbnsd,hnjd->bsh/dot_general | solution.py:71
  576.7 0.1 reduce-scatter.11.cloned.1.call-update
  576.8 6.9 %convolution_bitcast_fusion.2 = f32[1,1024,256]{2,1,0:T(8,128)} fusion(bf16[16,256,1024]{2,1,0:T(8,128)(2,1)} %all-gather.5.cloned.1.call-done, bf16[16,256,256]{2,1,0:T(8,128)(2,1)S(1)} %fusion.12), kind=kOutput, calls=%fused_computation.33 | convolution fusion | flops 2147483648 | bytes 11534336 | tf_op jit(solution)/shard_map/bsh,bsf->hf/dot_general | solution.py:49
  583.6 7.3 %convolution_bitcast_fusion.1 = f32[1,256,1024]{2,1,0:T(8,128)} fusion(bf16[16,256,1024]{2,1,0:T(8,128)(2,1)} %all-gather.9.cloned.1.call-done, f32[16,256,256]{2,1,0:T(8,128)S(1)} %copy-done.5), kind=kOutput, calls=%fused_computation.32 | convolution fusion | flops 2156920832 | bytes 13631488 | tf_op jit(solution)/shard_map/bsf,bsh->fh/dot_general | solution.py:46
  590.9 2.3 convolution_bitcast_fusion.3
  593.2 0.0 copy-start.3
  593.3 2.7 fusion.40
  596.0 75.7 %reduce-scatter.11.cloned.1.call-done = f32[16,16,1024]{2,1,0:T(8,128)} async-done(((f32[16,256,1024]{2,1,0:T(8,128)}), f32[16,16,1024]{2,1,0:T(8,128)}) %reduce-scatter.11.cloned.1.call-update) | async-done | bytes 1048592 | tf_op jit(solution)/shard_map/reduce_scatter | solution.py:27
  671.7 1.4 multiply_reduce_fusion.2
  673.1 2.5 subtract_add_fusion
  (42 shorter events, 0.1 us)
Async XLA Ops:
  7.2 69.9 %copy-start = (bf16[1,256,1024]{2,1,0:T(8,128)(2,1)S(1)}, bf16[1,256,1024]{2,1,0:T(8,128)(2,1)}, u32[]{:S(2)}) copy-start(bf16[1,256,1024]{2,1,0:T(8,128)(2,1)} %param.15) | copy-start | bytes 1572868
  7.2 62.0 %all-gather.5.cloned.1.call-start = ((), (), s32[]{:S(2)}) async-start(), calls=%async_computation.4 | async-start | bytes 8912896 | tf_op jit(solution)/shard_map/all_gather | solution.py:23
  11.5 168.9 %reduce-scatter.5.cloned.1.call-start = ((), (), s32[]{:S(2)}) async-start(), calls=%async_computation.5 | async-start | bytes 17825792 | tf_op jit(solution)/shard_map/reduce_scatter | solution.py:27
  75.1 1.9 copy-start.4
  85.4 1.2 copy-start.8
  85.4 95.0 %copy-start.11 = (f32[16,16,1024]{2,1,0:T(8,128)S(1)}, f32[16,16,1024]{2,1,0:T(8,128)}, u32[]{:S(2)}) copy-start(f32[16,16,1024]{2,1,0:T(8,128)} %param.9) | copy-start | bytes 3145732
  85.5 149.4 %all-gather.9.cloned.1.call-start = ((), (), s32[]{:S(2)}) async-start(), calls=%async_computation.8 | async-start | bytes 8912896 | tf_op jit(solution)/shard_map/all_gather | solution.py:23
  87.6 200.5 %all-gather.7.cloned.1.call-start = ((), (), s32[]{:S(2)}) async-start(), calls=%async_computation.6 | async-start | bytes 8912896 | tf_op jit(solution)/shard_map/all_gather | solution.py:23
  181.9 1.0 copy-start.2
  183.8 61.1 %copy-start.12 = (bf16[1,1024,256]{2,1,0:T(8,128)(2,1)S(1)}, bf16[1,1024,256]{2,1,0:T(8,128)(2,1)}, u32[]{:S(2)}) copy-start(bf16[1,1024,256]{2,1,0:T(8,128)(2,1)} %param.14) | copy-start | bytes 1572868
  183.8 201.3 %reduce-scatter.9.cloned.1.call-start = ((), (), s32[]{:S(2)}) async-start(), calls=%async_computation.9 | async-start | bytes 17825792 | tf_op jit(solution)/shard_map/reduce_scatter | solution.py:27
  253.0 35.0 %copy-start.16 = (bf16[1,1024,1,3,64]{1,4,3,2,0:T(8,128)(2,1)S(1)}, bf16[1,1024,1,3,64]{1,4,3,2,0:T(8,128)(2,1)}, u32[]{:S(2)}) copy-start(bf16[1,1024,1,3,64]{1,4,3,2,0:T(8,128)(2,1)} %param.12) | copy-start | bytes 1179652
  253.1 230.2 %reduce-scatter.7.cloned.1.call-start = ((), (), s32[]{:S(2)}) async-start(), calls=%async_computation.7 | async-start | bytes 17825792 | tf_op jit(solution)/shard_map/reduce_scatter | solution.py:27
  294.3 3.9 copy-start.10
  298.2 2.0 copy-start.6
  298.2 2.0 copy-start.19
  298.2 2.0 copy-start.13
  308.3 175.0 %copy-start.18 = (f32[16,16]{1,0:T(8,128)S(1)}, f32[16,16]{1,0:T(8,128)}, u32[]{:S(2)}) copy-start(f32[16,16]{1,0:T(8,128)} %get-tuple-element.15) | copy-start | bytes 3076
  308.4 231.3 %all-gather.11.cloned.1.call-start = ((), (), s32[]{:S(2)}) async-start(), calls=%async_computation.10 | async-start | bytes 8912896 | tf_op jit(solution)/shard_map/all_gather | solution.py:23
  487.3 184.4 %reduce-scatter.11.cloned.1.call-start = ((), (), s32[]{:S(2)}) async-start(), calls=%async_computation.11 | async-start | bytes 17825792 | tf_op jit(solution)/shard_map/reduce_scatter | solution.py:27
  539.7 6.2 copy-start.7
  576.7 6.9 %copy-start.5 = (f32[16,256,256]{2,1,0:T(8,128)S(1)}, f32[16,256,256]{2,1,0:T(8,128)}, u32[]{:S(2)}) copy-start(f32[16,256,256]{2,1,0:T(8,128)} %copy-done.4) | copy-start | bytes 12582916
  576.7 14.2 %slice-start = ((s8[8388608]{0:T(1024)(128)(4,1)}), s8[4194304]{0:T(1024)(128)(4,1)S(1)}, s32[]{:S(2)}) async-start(s8[8388608]{0:T(1024)(128)(4,1)} %bitcast.101), calls=%async_computation.12 | async-start | bytes 8388608
  576.8 16.5 %slice-start.2 = ((s8[8388608]{0:T(1024)(128)(4,1)}), s8[4194304]{0:T(1024)(128)(4,1)S(1)}, s32[]{:S(2)}) async-start(s8[8388608]{0:T(1024)(128)(4,1)} %bitcast.103), calls=%async_computation.14 | async-start | bytes 8388608
  583.6 7.3 %slice-start.1 = ((s8[8388608]{0:T(1024)(128)(4,1)}), s8[4194304]{0:T(1024)(128)(4,1)S(1)}, s32[]{:S(2)}) async-start(s8[8388608]{0:T(1024)(128)(4,1)} %bitcast.101), calls=%async_computation.13 | async-start | bytes 8388608
  583.6 9.6 %slice-start.3 = ((s8[8388608]{0:T(1024)(128)(4,1)}), s8[4194304]{0:T(1024)(128)(4,1)S(1)}, s32[]{:S(2)}) async-start(s8[8388608]{0:T(1024)(128)(4,1)} %bitcast.103), calls=%async_computation.15 | async-start | bytes 8388608
  590.9 2.3 copy-start.14
  590.9 2.3 copy-start.15
  593.2 78.5 %copy-start.3 = (f32[16,16,1024]{2,1,0:T(8,128)S(1)}, f32[16,16,1024]{2,1,0:T(8,128)}, u32[]{:S(2)}) copy-start(f32[16,16,1024]{2,1,0:T(8,128)} %copy-done.2) | copy-start | bytes 3145732
  593.3 79.9 %copy-start.9 = (f32[16,16,1024]{2,1,0:T(8,128)S(1)}, f32[16,16,1024]{2,1,0:T(8,128)}, u32[]{:S(2)}) copy-start(f32[16,16,1024]{2,1,0:T(8,128)} %param.11) | copy-start | bytes 3145732
  593.3 79.9 %copy-start.17 = (f32[16,16]{1,0:T(8,128)S(1)}, f32[16,16]{1,0:T(8,128)}, u32[]{:S(2)}) copy-start(f32[16,16]{1,0:T(8,128)} %get-tuple-element.13) | copy-start | bytes 3076
  593.3 82.3 %copy-start.1 = (bf16[1,256,1024]{2,1,0:T(8,128)(2,1)S(1)}, bf16[1,256,1024]{2,1,0:T(8,128)(2,1)}, u32[]{:S(2)}) copy-start(bf16[1,256,1024]{2,1,0:T(8,128)(2,1)} %param.15) | copy-start | bytes 1572868
Sparse Core Ops, SparseCore 0:
  11.6 57.5 all-gather.4
  85.6 94.8 reduce-scatter.4
  182.7 52.1 all-gather.8
  237.0 51.0 all-gather.6
  290.2 94.8 reduce-scatter.8
  387.3 95.9 reduce-scatter.6
  487.5 52.1 all-gather.10
  576.9 94.8 reduce-scatter.10
where the time goes:
time: 683 us; the launch traced here: 682 us
  waiting for transfers between devices  538 us (79%)
  matrix products  104 us (15%)
  other arithmetic  20.7 us (3%)
  between operations  14.4 us (2%)
    reduce_scatter x4, waiting for transfers between devices, scatter_positions(): return lax.psum_scatter(tensor, 'tp', scatter_dimension=1, tiled=True)  342 us
    all_gather x4, waiting for transfers between devices, gather_positions(): return lax.all_gather(tensor, 'tp', axis=1, tiled=True)  196 us
  transfers between devices with their start and end apart: 8, of which 8 were waited for; matrix products, arithmetic and copies ran while one was open for 9% of the time, Pallas kernels for 0%

commit v1 on v0

v1 whole, which is shorter than its diff:
```python
import jax
import jax.numpy as jnp
from jax import lax
from jax.sharding import PartitionSpec as P

RMS_EPS = 1e-6


def rms_norm(tensor):
    return tensor * lax.rsqrt(jnp.mean(tensor * tensor, axis=-1, keepdims=True) + RMS_EPS)


def rms_back(tensor, grad_in):
    inv_rms = lax.rsqrt(jnp.mean(tensor * tensor, axis=-1, keepdims=True) + RMS_EPS)
    return inv_rms * grad_in - tensor * (inv_rms * inv_rms * inv_rms) * jnp.mean(grad_in * tensor, axis=-1, keepdims=True)


def gelu_tanh(tensor):
    return jax.nn.gelu(tensor, approximate=True)


def gather(tensor):
    return lax.all_gather(tensor, "tp", axis=0, tiled=False)


def dot32(spec, left, right):
    return jnp.einsum(spec, left, right, preferred_element_type=jnp.float32)


def layer_backward(y_one, y_two, dy_one, dy_two, wq, wo, wu, wd):
    seqs, own, hidden = y_one.shape
    n_loc, dim = wo.shape[0], wo.shape[1]
    attn_scale = dim ** -0.5
    toks = seqs * own
    flat = lambda t: t.reshape(toks, hidden)

    u_mlp = flat(rms_norm(y_one).astype(jnp.bfloat16))
    cot_mlp = flat(dy_two.astype(jnp.bfloat16))
    wu_all = gather(wu)
    wd_all = gather(wd)
    u_all = gather(u_mlp)
    c_all = gather(cot_mlp)
    wq_all = gather(wq.reshape(hidden, n_loc * 3 * dim).T)
    wo_all = gather(wo.reshape(n_loc * dim, hidden))

    pre = dot32("tk,dkf->dtf", u_mlp, wu_all)
    hid, pull = jax.vjp(gelu_tanh, pre)
    g_out = dot32("dtf,dfh->th", hid.astype(jnp.bfloat16), wd_all)
    x_two = y_two - g_out.reshape(y_two.shape)
    d_pre = pull(dot32("th,dfh->dtf", cot_mlp, wd_all))[0].astype(jnp.bfloat16)
    du_mlp = dot32("dtf,dkf->tk", d_pre, wu_all)
    dy_one = dy_one + rms_back(y_one, du_mlp.reshape(y_one.shape))

    u_att = rms_norm(x_two).astype(jnp.bfloat16)
    cot_att = dy_one.astype(jnp.bfloat16)
    ua_all = gather(flat(u_att))
    ca_all = gather(flat(cot_att))
    n_dev = ua_all.shape[0]
    every = n_dev * toks

    u_all = u_all.reshape(every, hidden)
    c_all = c_all.reshape(every, hidden)
    pre_c = dot32("tk,kf->tf", u_all, wu)
    hid_c, pull_c = jax.vjp(gelu_tanh, pre_c)
    g_down = dot32("tf,th->fh", hid_c.astype(jnp.bfloat16), c_all)
    d_pre_c = pull_c(dot32("th,fh->tf", c_all, wd))[0].astype(jnp.bfloat16)
    g_up = dot32("tk,tf->kf", u_all, d_pre_c)

    ua_all = ua_all.reshape(every, hidden)
    ca_all = ca_all.reshape(every, hidden)

    def by_seq(t, width):
        return t.reshape(n_dev, seqs, own, n_loc, width).transpose(1, 3, 0, 2, 4).reshape(seqs, n_loc, n_dev * own, width)

    def by_dev(t):
        return t.reshape(seqs, n_loc, n_dev, own, dim).transpose(2, 0, 3, 1, 4).reshape(n_dev, toks, n_loc, dim)

    qkv = [by_seq(dot32("th,hc->tc", ua_all, wq[:, :, j].reshape(hidden, n_loc * dim)).astype(jnp.bfloat16), dim) for j in range(3)]
    q, k, v = qkv
    d_ctx = by_seq(dot32("th,ch->tc", ca_all, wo.reshape(n_loc * dim, hidden)).astype(jnp.bfloat16), dim)
    scores = dot32("bnqd,bnkd->bnqk", q, k) * attn_scale
    prob = jax.nn.softmax(scores, axis=-1)
    prob_b = prob.astype(jnp.bfloat16)
    ctx = dot32("bnqk,bnkd->bnqd", prob_b, v).astype(jnp.bfloat16)
    d_prob = dot32("bnqd,bnkd->bnqk", d_ctx, v)
    d_v = dot32("bnqk,bnqd->bnkd", prob_b, d_ctx).astype(jnp.bfloat16)
    d_s = (prob * (d_prob - jnp.sum(d_prob * prob, axis=-1, keepdims=True)) * attn_scale).astype(jnp.bfloat16)
    d_q = dot32("bnqk,bnkd->bnqd", d_s, k).astype(jnp.bfloat16)
    d_k = dot32("bnqk,bnqd->bnkd", d_s, q).astype(jnp.bfloat16)

    mine = jnp.stack([by_dev(t) for t in (ctx, d_q, d_k, d_v)], axis=3)
    c_head = mine[:, :, :, 0].reshape(every, n_loc * dim)
    d_head = mine[:, :, :, 1:].reshape(every, n_loc * 3 * dim)
    g_out_w = dot32("tc,th->ch", c_head, ca_all)
    g_qkv = dot32("th,tc->hc", ua_all, d_head)
    packed = lax.all_to_all(mine.reshape(n_dev, toks, n_loc * 4 * dim), "tp", 0, 0, tiled=False)
    packed = packed.reshape(n_dev, toks, n_loc, 4, dim)
    c_tok = packed[:, :, :, 0].reshape(n_dev, toks, n_loc * dim)
    d_tok = packed[:, :, :, 1:].reshape(n_dev, toks, n_loc * 3 * dim)
    f_out = dot32("dtc,dch->th", c_tok, wo_all)
    x_one = y_one - f_out.reshape(y_one.shape)
    du_att = dot32("dtc,dch->th", d_tok, wq_all)
    dx_two = dy_two + rms_back(x_two, du_att.reshape(x_two.shape))
    return x_one, x_two, dy_one, dx_two, g_qkv.reshape(wq.shape), g_out_w.reshape(wo.shape), g_up, g_down


def local_backward(y_one, y_two, dy_one, dy_two, w_qkv, w_out, w_up, w_down):
    grads = []
    state = (y_one, y_two, dy_one, dy_two)
    for idx in reversed(range(w_qkv.shape[0])):
        res = layer_backward(*state, w_qkv[idx], w_out[idx], w_up[idx], w_down[idx])
        state = res[:4]
        grads.append(res[4:])
    return state + tuple(jnp.stack(g[::-1]) for g in zip(*grads))


def solution(mesh):
    state_spec = P("dp", "tp", None)
    in_specs = (state_spec, state_spec, state_spec, state_spec, P(None, None, "tp", None, None), P(None, "tp", None, None), P(None, None, "tp"), P(None, "tp", None))
    out_specs = (state_spec, state_spec, state_spec, state_spec, P("dp", None, "tp", None, None), P("dp", "tp", None, None), P("dp", None, "tp"), P("dp", "tp", None))
    return jax.shard_map(local_backward, mesh=mesh, in_specs=in_specs, out_specs=out_specs, check_vma=False)
```

time: 683 us -> 472 us (0.69)
  waiting for transfers between devices: 538 us -> 248 us
  local copies, waits for them, and re-layouts: 4.85 us -> 45.7 us
  matrix products: 104 us -> 134 us
    reduce_scatter x4 -> x0, waiting for transfers between devices: 342 us -> none  [scatter_positions(): return lax.psum_scatter(tensor, 'tp', scatter_dimension=1, tiled=True)]
    all_gather x4 -> x8, waiting for transfers between devices: 196 us -> 230 us  [gather(): return lax.all_gather(tensor, 'tp', axis=0, tiled=False)]
    dot_general x18 -> x19, matrix products: 104 us -> 129 us  [dot32(): return jnp.einsum(spec, left, right, preferred_element_type=jnp.float32)]
    all_to_all x0 -> x1, waiting for transfers between devices: none -> 15.7 us  [layer_backward(): lax.all_to_all(mine.reshape(n_dev, toks, n_loc * 4 * dim), 'tp', 0, 0, ti...]
    convert_element_type x0 -> x8, local copies, waits for them, and re-layouts: none -> 13.1 us  [the longest x3 4.7 us: layer_backward(): dot32('th,hc->tc', ua_all, wq[:, :, j].reshape(hidden, n_loc * dim))]
    transpose x0 -> x8, local copies, waits for them, and re-layouts: none -> 10.3 us  [the longest x4 5.27 us: by_dev(): t.reshape(seqs, n_loc, n_dev, own, dim).transpose(2, 0, 3, 1, 4)]
    another operation x0 -> x2, local copies, waits for them, and re-layouts: none -> 9.84 us  [layer_backward(): mine = jnp.stack([by_dev(t) for t in (ctx, d_q, d_k, d_v)], axis=3)]
    dot_general x0 -> x3, local copies, waits for them, and re-layouts: none -> 7.45 us  [dot32(): return jnp.einsum(spec, left, right, preferred_element_type=jnp.float32)]
  transfers between devices with their start and end apart: 8 -> 9, of which waited for: 8 -> 7; matrix products, arithmetic and copies ran while one was open for 9% -> 41% of each run, Pallas kernels for 0% -> 0%
where the time goes in v1:
time: 472 us; the launch traced here: 465 us
  waiting for transfers between devices  248 us (53%)
  matrix products  134 us (28%)
  local copies, waits for them, and re-layouts  45.7 us (10%)
  other arithmetic  16.1 us (3%)
  between operations  14.8 us (3%)
  starting transfers between devices  6.24 us (1%)
    all_gather x8, waiting for transfers between devices, gather(): return lax.all_gather(tensor, 'tp', axis=0, tiled=False)  230 us
    dot_general x19, matrix products, dot32(): return jnp.einsum(spec, left, right, preferred_element_type=jnp.float32)  129 us
    all_to_all x1, waiting for transfers between devices, layer_backward(): lax.all_to_all(mine.reshape(n_dev, toks, n_loc * 4 * dim), 'tp', 0, 0, ti...  15.7 us
    another operation x2, local copies, waits for them, and re-layouts, layer_backward(): mine = jnp.stack([by_dev(t) for t in (ctx, d_q, d_k, d_v)], axis=3)  9.84 us
  transfers between devices with their start and end apart: 9, of which 7 were waited for; matrix products, arithmetic and copies ran while one was open for 41% of the time, Pallas kernels for 0%

profile of v1, /device:TPU:21, one launch (start us, length us, event | category | flops | bytes accessed | tf_op | source)
XLA Modules:
  0.0 464.9 jit_solution(18117397173563940809)
XLA Ops:
  7.2 0.7 all-gather.11.cloned.1.call-update
  8.0 0.7 all-gather.13.cloned.1.call-update
  8.9 1.4 multiply_reduce_fusion.5
  10.2 2.1 multiply_convert_fusion.6
  12.5 54.7 %all-gather.11.cloned.1.call-done = bf16[16,1024,256]{2,1,0:T(8,128)(2,1)} async-done(((bf16[1,1024,256]{2,1,0:T(8,128)(2,1)}), bf16[16,1024,256]{2,1,0:T(8,128)(2,1)}) %all-gather.11.cloned.1.call-update) | async-done | bytes 8388624 | tf_op jit(solution)/shard_map/all_gather | solution.py:23
  67.2 8.0 %fusion.113 = f32[256,16,256]{2,0,1:T(8,128)} fusion(bf16[256,1024,1]{1,0,2:T(8,128)(2,1)} %bitcast.225, bf16[16,1024,256]{2,1,0:T(8,128)(2,1)} %all-gather.11.cloned.1.call-done), kind=kOutput, calls=%fused_computation.127 | convolution fusion | flops 2147483648 | bytes 13107200 | tf_op jit(solution)/shard_map/tk,dkf->dtf/dot_general | solution.py:27
  75.2 44.7 %all-gather.13.cloned.1.call-done = bf16[16,256,1024]{2,1,0:T(8,128)(2,1)} async-done(((bf16[1,256,1024]{2,1,0:T(8,128)(2,1)}), bf16[16,256,1024]{2,1,0:T(8,128)(2,1)}) %all-gather.13.cloned.1.call-update) | async-done | bytes 8388624 | tf_op jit(solution)/shard_map/all_gather | solution.py:23
  119.9 7.4 %fusion.33 = f32[256,1024,1]{1,0,2:T(8,128)S(1)} fusion(bf16[16,256,1024]{2,1,0:T(8,128)(2,1)} %all-gather.13.cloned.1.call-done, f32[256,16,256]{2,0,1:T(8,128)} %fusion.113), kind=kOutput, calls=%fused_computation.43 | convolution fusion | flops 2156920832 | bytes 13631488 | tf_op jit(solution)/shard_map/dtf,dfh->th/dot_general | solution.py:27
  127.5 0.9 multiply_convert_fusion.5
  128.7 0.9 convert_element_type.68
  129.6 11.0 %fusion.52 = f32[256,1024,1]{1,0,2:T(8,128)S(1)} fusion(bf16[16,1024,256]{2,1,0:T(8,128)(2,1)} %all-gather.11.cloned.1.call-done, f32[256,16,256]{2,0,1:T(8,128)} %fusion.113, bf16[16,256,1024]{2,1,0:T(8,128)(2,1)} %all-gather.13.cloned.1.call-done, bf16[256,1024,1]{1,0,2:T(8,128)(2,1)} %bitcast.222), kind=kOutput, calls=%fused_computation.61 | convolution fusion | flops 4315938816 | bytes 22544384 | tf_op jit(solution)/shard_map/dtf,dkf->tk/dot_general | solution.py:27
  140.8 2.6 fusion.111
  143.5 0.6 all-gather.21.cloned.1.call-update
  144.2 0.7 all-gather.25.cloned.1.call-update
  144.9 0.5 all-gather.23.cloned.1.call-start
  145.7 27.4 %all-gather.19.cloned.1.call-done = bf16[16,256,1024]{2,1,0:T(8,128)(2,1)} async-done(((bf16[1,256,1024]{2,1,0:T(8,128)(2,1)}), bf16[16,256,1024]{2,1,0:T(8,128)(2,1)}) %all-gather.19.cloned.1.call-update) | async-done | bytes 8388624 | tf_op jit(solution)/shard_map/all_gather | solution.py:23
  173.2 7.8 %fusion.75 = f32[4096,256]{1,0:T(8,128)} fusion(bf16[4096,1024]{1,0:T(8,128)(2,1)} %bitcast.239, bf16[1,1024,256]{2,1,0:T(8,128)(2,1)} %param.14), kind=kOutput, calls=%fused_computation.85 | convolution fusion | flops 2147483648 | bytes 13107200 | tf_op jit(solution)/shard_map/tk,kf->tf/dot_general | solution.py:27
  181.0 45.3 %all-gather.15.cloned.1.call-done = bf16[16,256,1024]{2,1,0:T(8,128)(2,1)} async-done(((bf16[1,256,1024]{2,1,0:T(8,128)(2,1)}), bf16[16,256,1024]{2,1,0:T(8,128)(2,1)}) %all-gather.15.cloned.1.call-update) | async-done | bytes 8388624 | tf_op jit(solution)/shard_map/all_gather | solution.py:23
  226.3 7.0 %convolution_convert_fusion.3 = bf16[4096,64]{0,1:T(8,128)(2,1)} fusion(bf16[4096,1024]{1,0:T(8,128)(2,1)} %bitcast.190, bf16[1024,1,3,64]{0,3,2,1:T(8,128)(2,1)S(1)} %bitcast.229), kind=kOutput, calls=%fused_computation.9 | convolution fusion | flops 537133056 | bytes 9043968 | tf_op jit(solution)/shard_map/th,hc->tc/dot_general | solution.py:27
  233.3 3.5 convolution_convert_fusion.2
  236.8 3.5 convolution_convert_fusion.1
  240.2 39.2 %all-gather.17.cloned.1.call-done = bf16[16,256,1024]{2,1,0:T(8,128)(2,1)} async-done(((bf16[1,256,1024]{2,1,0:T(8,128)(2,1)}), bf16[16,256,1024]{2,1,0:T(8,128)(2,1)}) %all-gather.17.cloned.1.call-update) | async-done | bytes 8388624 | tf_op jit(solution)/shard_map/all_gather | solution.py:23
  279.4 6.8 %convolution_convert_fusion = bf16[4096,64]{0,1:T(8,128)(2,1)} fusion(bf16[4096,1024]{1,0:T(8,128)(2,1)} %bitcast.194, bf16[1,1,64,1024]{3,2,1,0:T(8,128)(2,1)S(1)} %copy-done.13), kind=kOutput, calls=%fused_computation.6 | convolution fusion | flops 537133056 | bytes 9043968 | tf_op jit(solution)/shard_map/th,ch->tc/dot_general | solution.py:27
  286.3 1.5 copy.109
  287.8 1.2 copy.110
  289.0 1.5 copy.96
  290.6 1.2 copy.97
  291.8 1.7 copy.98
  293.5 1.2 copy.99
  294.8 1.5 copy.102
  296.3 1.2 copy.103
  297.5 5.1 %fusion.112 = (f32[16,256]{1,0:T(8,128)S(1)}, f32[16,256,256]{1,2,0:T(8,128)}) fusion(bf16[16,256,64]{2,1,0:T(8,128)(2,1)} %bitcast.235, bf16[16,256,64]{2,1,0:T(8,128)(2,1)} %bitcast.237), kind=kOutput, calls=%fused_computation.126 | convolution fusion | flops 137363712 | bytes 5259264 | tf_op jit(solution)/shard_map/sub | solution.py:82
  302.6 4.0 fusion.114
  306.7 1.6 convolution_convert_fusion.4
  308.2 8.9 %fusion.69 = bf16[16,256,64]{1,2,0:T(8,128)(2,1)} fusion(bf16[16,256,64]{2,1,0:T(8,128)(2,1)} %bitcast.236, f32[16,256,256]{1,2,0:T(8,128)} %fusion.114, f32[16,256,256]{1,2,0:T(8,128)} %get-tuple-element.17, f32[16,256]{1,0:T(8,128)S(1)} %get-tuple-element.16), kind=kOutput, calls=%fused_computation.68 | convolution fusion | flops 141824256 | bytes 9453568 | tf_op jit(solution)/shard_map/bnqk,bnqd->bnkd/dot_general | solution.py:27
  317.1 8.7 %fusion.66 = bf16[16,256,64]{1,2,0:T(8,128)(2,1)} fusion(bf16[16,256,64]{2,1,0:T(8,128)(2,1)} %bitcast.238, f32[16,256,256]{1,2,0:T(8,128)} %fusion.114, f32[16,256,256]{1,2,0:T(8,128)} %get-tuple-element.17, f32[16,256]{1,0:T(8,128)S(1)} %get-tuple-element.16), kind=kOutput, calls=%fused_computation.67 | convolution fusion | flops 141824256 | bytes 9453568 | tf_op jit(solution)/shard_map/bnqk,bnkd->bnqd/dot_general | solution.py:27
  325.9 3.5 convolution_convert_fusion.5
  329.4 1.5 copy.123
  330.9 1.2 copy.124
  332.2 1.5 copy.119
  333.7 1.2 copy.120
  334.9 1.5 copy.115
  336.5 1.3 copy.116
  337.7 2.4 copy.106
  340.1 1.5 copy.107
  341.6 4.0 pad_maximum_fusion
  345.6 4.8 %copy.125 = bf16[16,256,1,4,64]{1,4,3,0,2:T(8,128)(2,1)} copy(bf16[16,256,1,4,64]{4,1,0,3,2:T(8,128)(2,1)} %pad_maximum_fusion) | data formatting | bytes 4194304 | tf_op jit(solution)/shard_map/stack | solution.py:91
  350.4 5.3 %all-to-all-start = ((bf16[16,256,256]{1,2,0:T(8,128)(2,1)}), bf16[16,256,256]{1,2,0:T(8,128)(2,1)}, u32[]{:S(2)}, u32[]{:S(2)}) async-start(bf16[16,256,256]{1,2,0:T(8,128)(2,1)} %bitcast.204), calls=%async_computation | async-start | bytes 4194304 | tf_op jit(solution)/shard_map/all_to_all | solution.py:96
  355.7 8.2 %fusion.62 = f32[1,256,1024]{2,1,0:T(8,128)} fusion(bf16[4096,1024]{1,0:T(8,128)(2,1)} %bitcast.241, f32[4096,256]{1,0:T(8,128)} %fusion.75), kind=kOutput, calls=%fused_computation.65 | convolution fusion | flops 2156920832 | bytes 13631488 | tf_op jit(solution)/shard_map/tf,th->fh/dot_general | solution.py:27
  363.8 17.3 %fusion.53 = f32[1,1024,256]{2,1,0:T(8,128)} fusion(bf16[4096,1024]{1,0:T(8,128)(2,1)} %bitcast.240, f32[4096,256]{1,0:T(8,128)} %fusion.75, bf16[4096,1024]{1,0:T(8,128)(2,1)} %bitcast.242, bf16[1,256,1024]{2,1,0:T(8,128)(2,1)} %param.15), kind=kOutput, calls=%fused_computation.62 | convolution fusion | flops 4315938816 | bytes 22544384 | tf_op jit(solution)/shard_map/tk,tf->kf/dot_general | solution.py:27
  381.1 5.8 %convolution_bitcast_fusion.1 = f32[1,1,64,1024]{3,2,1,0:T(8,128)} fusion(bf16[4096,64]{1,0:T(8,128)(2,1)S(1)} %bitcast.197, bf16[4096,1024]{1,0:T(8,128)(2,1)} %bitcast.195), kind=kOutput, calls=%fused_computation.72 | convolution fusion | flops 536870912 | bytes 9175040 | tf_op jit(solution)/shard_map/tc,th->ch/dot_general | solution.py:27
  387.0 2.5 pad_maximum_fusion.1
  389.4 5.1 %copy.130 = bf16[16,256,1,3,64]{1,0,4,3,2:T(8,128)(2,1)} copy(bf16[16,256,1,3,64]{4,1,0,3,2:T(8,128)(2,1)} %pad_maximum_fusion.1) | data formatting | bytes 3145728 | tf_op jit(solution)/shard_map/stack | solution.py:91
  394.5 2.1 copy.147
  396.6 6.1 %convolution_bitcast_fusion = f32[1,1024,1,3,64]{1,4,3,2,0:T(8,128)} fusion(bf16[4096,1024,1]{1,0,2:T(8,128)(2,1)} %bitcast.191, bf16[3,64,4096]{2,1,0:T(8,128)(2,1)S(1)} %bitcast.232), kind=kOutput, calls=%fused_computation.69 | convolution fusion | flops 1610612736 | bytes 10747904 | tf_op jit(solution)/shard_map/th,tc->hc/dot_general | solution.py:27
  402.7 15.7 %all-to-all-done = bf16[16,256,256]{1,2,0:T(8,128)(2,1)} async-done(((bf16[16,256,256]{1,2,0:T(8,128)(2,1)}), bf16[16,256,256]{1,2,0:T(8,128)(2,1)}, u32[]{:S(2)}, u32[]{:S(2)}) %all-to-all-start) | async-done | bytes 2097184 | tf_op jit(solution)/shard_map/all_to_all | solution.py:96
  418.3 2.7 slice.26
  421.1 1.1 slice_bitcast_fusion
  422.2 1.9 copy.126
  424.0 4.5 copy.128
  428.5 6.1 %multiply_reduce_fusion.2 = (f32[16,16]{1,0:T(8,128)S(1)}, f32[16,16,1024]{2,1,0:T(8,128)S(1)}) fusion(f32[16,16,1024]{2,1,0:T(8,128)S(1)} %get-tuple-element.9, bf16[16,192,1024,1]{2,1,0,3:T(8,128)(2,1)} %bitcast.243, bf16[16,16,192,16]{2,3,1,0:T(8,128)(2,1)} %bitcast.221), kind=kOutput, calls=%fused_computation.75 | convolution fusion | flops 1611136768 | bytes 9962496 | tf_op jit(solution)/shard_map/dtc,dch->th/dot_general | solution.py:27
  434.7 1.3 subtract_add_fusion
  436.0 18.2 %all-gather.23.cloned.1.call-done = bf16[16,1,64,1024]{3,2,1,0:T(8,128)(2,1)} async-done(((bf16[1,1,64,1024]{3,2,1,0:T(8,128)(2,1)}), bf16[16,1,64,1024]{3,2,1,0:T(8,128)(2,1)}) %all-gather.23.cloned.1.call-update) | async-done | bytes 2097168 | tf_op jit(solution)/shard_map/all_gather | solution.py:23
  454.2 3.5 fusion.63
  (49 shorter events, 1.5 us)
Async XLA Ops:
  7.2 60.0 %all-gather.11.cloned.1.call-start = ((), (), s32[]{:S(2)}) async-start(), calls=%async_computation.1 | async-start | bytes 8912896 | tf_op jit(solution)/shard_map/all_gather | solution.py:23
  8.0 111.9 %all-gather.13.cloned.1.call-start = ((), (), s32[]{:S(2)}) async-start(), calls=%async_computation.2 | async-start | bytes 8912896 | tf_op jit(solution)/shard_map/all_gather | solution.py:23
  8.8 164.4 %all-gather.19.cloned.1.call-start = ((), (), s32[]{:S(2)}) async-start(), calls=%async_computation.5 | async-start | bytes 8912896 | tf_op jit(solution)/shard_map/all_gather | solution.py:23
  12.4 213.9 %all-gather.15.cloned.1.call-start = ((), (), s32[]{:S(2)}) async-start(), calls=%async_computation.3 | async-start | bytes 8912896 | tf_op jit(solution)/shard_map/all_gather | solution.py:23
  75.2 52.1 %copy-start.11 = (f32[16,16,1024]{2,1,0:T(8,128)S(1)}, f32[16,16,1024]{2,1,0:T(8,128)}, u32[]{:S(2)}) copy-start(f32[16,16,1024]{2,1,0:T(8,128)} %param.9) | copy-start | bytes 3145732
  127.3 1.4 copy-start.6
  127.5 307.2 %copy-start.2 = (f32[16,16,1024]{2,1,0:T(8,128)}, f32[16,16,1024]{2,1,0:T(8,128)S(1)}, u32[]{:S(2)}) copy-start(f32[16,16,1024]{2,1,0:T(8,128)S(1)} %get-tuple-element.9) | copy-start | bytes 3145732
  128.5 150.9 %all-gather.17.cloned.1.call-start = ((), (), s32[]{:S(2)}) async-start(), calls=%async_computation.4 | async-start | bytes 8912896 | tf_op jit(solution)/shard_map/all_gather | solution.py:23
  129.6 11.0 %copy-start.1 = (f32[16,16,1024]{2,1,0:T(8,128)S(1)}, f32[16,16,1024]{2,1,0:T(8,128)}, u32[]{:S(2)}) copy-start(f32[16,16,1024]{2,1,0:T(8,128)} %param.8) | copy-start | bytes 3145732
  143.5 212.2 %all-gather.21.cloned.1.call-start = ((), (), s32[]{:S(2)}) async-start(), calls=%async_computation.6 | async-start | bytes 8912896 | tf_op jit(solution)/shard_map/all_gather | solution.py:23
  144.1 284.4 %all-gather.25.cloned.1.call-start = ((), (), s32[]{:S(2)}) async-start(), calls=%async_computation.8 | async-start | bytes 6684672 | tf_op jit(solution)/shard_map/all_gather | solution.py:23
  144.9 309.2 %all-gather.23.cloned.1.call-start = ((), (), s32[]{:S(2)}) async-start(), calls=%async_computation.7 | async-start | bytes 2228224 | tf_op jit(solution)/shard_map/all_gather | solution.py:23
  173.2 53.1 %copy-start.10 = (bf16[1,1024,1,3,64]{1,4,3,2,0:T(8,128)(2,1)S(1)}, bf16[1,1024,1,3,64]{1,4,3,2,0:T(8,128)(2,1)}, u32[]{:S(2)}) copy-start(bf16[1,1024,1,3,64]{1,4,3,2,0:T(8,128)(2,1)} %param.12) | copy-start | bytes 1179652
  226.3 7.0 %copy-start = (bf16[16,256,1024]{2,1,0:T(8,128)(2,1)S(1)}, bf16[16,256,1024]{2,1,0:T(8,128)(2,1)}, u32[]{:S(2)}) copy-start(bf16[16,256,1024]{2,1,0:T(8,128)(2,1)} %all-gather.15.cloned.1.call-done) | copy-start | bytes 25165828
  236.8 42.7 %copy-start.13 = (bf16[1,1,64,1024]{3,2,1,0:T(8,128)(2,1)S(1)}, bf16[1,1,64,1024]{3,2,1,0:T(8,128)(2,1)}, u32[]{:S(2)}) copy-start(bf16[1,1,64,1024]{3,2,1,0:T(8,128)(2,1)} %param.13) | copy-start | bytes 393220
  297.5 5.1 %copy-start.8 = (bf16[16,1,16,16,64]{4,3,2,0,1:T(8,128)(2,1)S(1)}, bf16[16,1,16,16,64]{4,3,2,0,1:T(8,128)(2,1)}, u32[]{:S(2)}) copy-start(bf16[16,1,16,16,64]{4,3,2,0,1:T(8,128)(2,1)} %copy.110) | copy-start | bytes 1572868
  302.6 4.0 copy-start.14
  317.1 8.7 %copy-start.9 = (bf16[16,1,16,16,64]{4,3,2,0,1:T(8,128)(2,1)S(1)}, bf16[16,1,16,16,64]{4,3,2,0,1:T(8,128)(2,1)}, u32[]{:S(2)}) copy-start(bf16[16,1,16,16,64]{4,3,2,0,1:T(8,128)(2,1)} %copy.103) | copy-start | bytes 1572868
  350.4 68.0 %all-to-all-start = ((bf16[16,256,256]{1,2,0:T(8,128)(2,1)}), bf16[16,256,256]{1,2,0:T(8,128)(2,1)}, u32[]{:S(2)}, u32[]{:S(2)}) async-start(bf16[16,256,256]{1,2,0:T(8,128)(2,1)} %bitcast.204), calls=%async_computation | async-start | bytes 4194304 | tf_op jit(solution)/shard_map/all_to_all | solution.py:96
  381.1 5.8 %copy-start.3 = (bf16[16,16,16,1,64]{4,2,1,0,3:T(8,128)(2,1)S(1)}, bf16[16,16,16,1,64]{4,2,1,0,3:T(8,128)(2,1)}, u32[]{:S(2)}) copy-start(bf16[16,16,16,1,64]{4,2,1,0,3:T(8,128)(2,1)} %copy.124) | copy-start | bytes 1572868
  381.1 5.8 %copy-start.4 = (bf16[16,16,16,1,64]{4,2,1,0,3:T(8,128)(2,1)S(1)}, bf16[16,16,16,1,64]{4,2,1,0,3:T(8,128)(2,1)}, u32[]{:S(2)}) copy-start(bf16[16,16,16,1,64]{4,2,1,0,3:T(8,128)(2,1)} %copy.120) | copy-start | bytes 1572868
  381.1 5.8 %copy-start.5 = (bf16[16,16,16,1,64]{4,2,1,0,3:T(8,128)(2,1)S(1)}, bf16[16,16,16,1,64]{4,2,1,0,3:T(8,128)(2,1)}, u32[]{:S(2)}) copy-start(bf16[16,16,16,1,64]{4,2,1,0,3:T(8,128)(2,1)} %copy.116) | copy-start | bytes 1572868
  428.5 6.2 %copy-start.7 = (f32[16,16,1024]{2,1,0:T(8,128)S(1)}, f32[16,16,1024]{2,1,0:T(8,128)}, u32[]{:S(2)}) copy-start(f32[16,16,1024]{2,1,0:T(8,128)} %param.11) | copy-start | bytes 3145732
  434.7 19.5 %copy-start.12 = (bf16[256,64,16]{1,2,0:T(8,128)(2,1)S(1)}, bf16[256,64,16]{1,2,0:T(8,128)(2,1)}, u32[]{:S(2)}) copy-start(bf16[256,64,16]{1,2,0:T(8,128)(2,1)} %copy.126) | copy-start | bytes 1572868
Sparse Core Ops, SparseCore 0:
  9.6 57.5 all-gather.10
  68.8 51.0 all-gather.12
  122.1 51.0 all-gather.18
  175.2 51.0 all-gather.14
  228.4 51.0 all-gather.16
  280.9 51.0 all-gather.20
  333.6 79.9 all-gather.24
  415.2 38.8 all-gather.22

commit v2 on v0

v2 whole, which is shorter than its diff:
```python
import functools

import jax
import jax.numpy as jnp
from jax import lax
from jax.experimental import pallas as pl
from jax.experimental.pallas import tpu as pltpu
from jax.sharding import PartitionSpec as P

RMS_EPS = 1e-6
MESH = pl.DeviceIdType.MESH
BF16 = jnp.bfloat16
F32 = jnp.float32


def dot_nn(a, b):
    return lax.dot_general(a, b, (((1,), (0,)), ((), ())), preferred_element_type=F32)


def dot_nt(a, b):
    return lax.dot_general(a, b, (((1,), (1,)), ((), ())), preferred_element_type=F32)


def dot_tn(a, b):
    return lax.dot_general(a, b, (((0,), (0,)), ((), ())), preferred_element_type=F32)


def inv_rms(x):
    return lax.rsqrt(jnp.mean(x * x, axis=-1, keepdims=True) + RMS_EPS)


def rms_back(x, g):
    r = inv_rms(x)
    return r * g - x * (r * r * r) * jnp.mean(g * x, axis=-1, keepdims=True)


def activation(a, e):
    c0, c1 = 0.7978845608028654, 0.044715
    t = jnp.tanh(c0 * (a + c1 * (a * a * a)))
    half = 0.5 * (1.0 + t)
    slope = half + (0.5 * a) * ((1.0 + t) * (1.0 - t)) * (c0 * (1.0 + (3.0 * c1) * (a * a)))
    return (a * half).astype(BF16), (slope * e).astype(BF16)


class Ring:
    def __init__(self, place, buf, pieces, sems):
        self.place, self.buf, self.pieces = place, buf, pieces
        self.send_l, self.recv_l, self.send_s, self.recv_s, self.send_m, self.recv_m = sems

    def at(self, dev, p):
        j, row, rows = self.pieces[p]
        return self.buf.at[dev, j, pl.ds(row, rows)]

    def copy(self, dev, p, send, recv, to, src=None):
        ref = self.at(dev, p)
        return pltpu.make_async_remote_copy(
            src_ref=ref if src is None else src, dst_ref=ref, send_sem=send, recv_sem=recv,
            device_id={"tp": to}, device_id_type=MESH)

    def long(self, p, k):
        pc = self.place
        return self.copy(pc.slot(-k, 0), p, self.send_l.at[p, k], self.recv_l.at[p, k], pc.long_dev)

    def short(self, p, k):
        pc = self.place
        return self.copy(pc.slot(k, 0), p, self.send_s.at[p, k], self.recv_s.at[p, k], pc.short_dev)

    def start_own(self, p):
        pc = self.place
        self.long(p, 0).start()
        self.short(p, 0).start()
        self.copy(pc.me, p, self.send_m.at[p, 0], self.recv_m.at[p, 0], pc.mate).start()

    def step_long(self, p, k, forward=True):
        pc = self.place
        dev = pc.slot(-k, 0)
        self.copy(dev, p, self.send_l.at[p, k - 1], self.recv_l.at[p, k - 1], pc.long_dev).wait_recv()
        if forward:
            self.long(p, k).start()
        self.copy(dev, p, self.send_m.at[p, k], self.recv_m.at[p, k], pc.mate).start()

    def step_short(self, p, k, forward=True):
        pc = self.place
        dev = pc.slot(k, 0)
        far = pc.far
        self.copy(dev, p, self.send_s.at[p, k - 1], self.recv_s.at[p, k - 1], pc.short_dev).wait_recv()
        if forward is True:
            self.short(p, k).start()
        elif forward is not False:
            @pl.when(forward)
            def _():
                self.short(p, k).start()
        self.copy(dev, p, self.send_m.at[p, far + k], self.recv_m.at[p, far + k], pc.mate).start()

    def mate_own(self, p):
        pc = self.place
        self.copy(pc.mate, p, self.send_m.at[p, 0], self.recv_m.at[p, 0], pc.mate).wait_recv()

    def mate_long(self, p, k):
        pc = self.place
        self.copy(pc.slot(k, 1), p, self.send_m.at[p, k], self.recv_m.at[p, k], pc.mate).wait_recv()

    def mate_short(self, p, k):
        pc = self.place
        self.copy(pc.slot(-k, 1), p, self.send_m.at[p, pc.far + k], self.recv_m.at[p, pc.far + k], pc.mate).wait_recv()

    def drain(self):
        pc = self.place
        for p in range(len(self.pieces)):
            for k in range(pc.far):
                self.long(p, k).wait_send()
            for k in range(pc.far - 1):
                self.short(p, k).wait_send()
            for k in range(2 * pc.far):
                self.copy(pc.me, p, self.send_m.at[p, k], self.recv_m.at[p, k], pc.mate).wait_send()


class Place:
    def __init__(self, n_dev):
        self.n_dev, self.n_chip = n_dev, n_dev // 2
        self.far = self.n_chip // 2
        self.me = lax.axis_index("tp")
        self.chip, self.core = self.me // 2, lax.rem(self.me, 2)
        self.sign = 1 - 2 * self.core
        self.mate = 2 * self.chip + 1 - self.core
        self.long_dev = self.slot(1, 0)
        self.short_dev = self.slot(-1, 0)

    def slot(self, hops, other):
        chip = lax.rem(self.chip + hops * self.sign + self.n_chip, self.n_chip)
        return 2 * chip + (1 - self.core if other else self.core)


def kernel(n_dev, seqs, own, dim, scale,
           y1, y2, dy1, dy2, w1, w2, wo, wq,
           x1, x2, dyo, dx2, gq, go, gw1, gw2,
           xa, xb, w4, stage, packed, uc, w1t, w1raw, acc0, acc1, accw,
           a_sems, b_sems, c_sems, d_sems, load_sem, all_send, all_recv, free_sem):
    pc = Place(n_dev)
    me = pc.me
    toks = seqs * own
    hidden = y1.shape[1]
    group = seqs // 4
    far = pc.far

    loads = [(y1, x1), (dy2, dx2), (y2, x2), (dy1, dyo), (w2, xa.at[me, 1]), (w1, w1raw),
             (wo, w4.at[me, 0, pl.ds(0, dim)]), (wq.at[0], w4.at[me, 0, pl.ds(dim, dim)]),
             (wq.at[2], w4.at[me, 0, pl.ds(2 * dim, dim)]), (wq.at[1], w4.at[me, 0, pl.ds(3 * dim, dim)])]
    loads = [pltpu.make_async_copy(src, dst, load_sem.at[i]) for i, (src, dst) in enumerate(loads)]
    for i in (4, 5, 0, 1, 2, 3, 6, 7, 8, 9):
        loads[i].start()

    barrier = pltpu.get_barrier_semaphore()
    for hop in range(1, n_dev):
        pl.semaphore_signal(barrier, inc=1, device_id={"tp": lax.rem(me + hop, n_dev)}, device_id_type=MESH)
    pl.semaphore_wait(barrier, n_dev - 1)

    half = toks // 2
    ring_a = Ring(pc, xa, [(1, 0, toks), (0, 0, toks)], a_sems)
    ring_b = Ring(pc, xb, [(0, 0, half), (1, 0, half), (0, half, half), (1, half, half)], b_sems)
    ring_d = Ring(pc, w4, [(0, 0, 4 * dim)], d_sems)
    ring_c = Ring(pc, xa, [(0, 0, toks), (1, 0, toks)], c_sems)

    loads[4].wait()
    ring_a.start_own(0)
    loads[5].wait()
    turned = w1raw[...].T
    w1t[...] = turned
    xa[me, 0] = turned
    loads[0].wait()
    loads[1].wait()

    def norm_rows(i, _):
        rows = pl.ds(pl.multiple_of(i * 64, 64), 64)
        t = x1[rows]
        uc[0, rows] = (t * inv_rms(t)).astype(BF16)
        uc[1, rows] = dx2[rows].astype(BF16)
        return 0

    ring_a.start_own(1)
    lax.fori_loop(0, toks // 64, norm_rows, 0)
    acc0[...] = jnp.zeros_like(acc0)
    acc1[...] = jnp.zeros_like(acc1)
    for i in (2, 3, 6, 7, 8, 9):
        loads[i].wait()

    def mlp_rows(d):
        left, right = xa[d, 0], xa[d, 1]
        h, da = activation(dot_nt(uc[0], left), dot_nt(uc[1], right))
        acc0[...] += dot_nn(h, right)
        acc1[...] += dot_nn(da, left)

    def pair(chip_hops, body):
        chip = lax.rem(pc.chip + chip_hops + pc.n_chip, pc.n_chip)
        lax.fori_loop(0, 2, lambda i, _: (body(2 * chip + i), 0)[1], 0)

    def four(k, body):
        def one(i, _):
            chip = lax.rem(pc.chip + k * (1 - 2 * (i // 2)) + pc.n_chip, pc.n_chip)
            body(2 * chip + lax.rem(i, 2))
            return 0
        lax.fori_loop(0, 4, one, 0)

    def mates(ring, k, last):
        for p in range(len(ring.pieces)):
            ring.mate_long(p, k)
            if not last:
                ring.mate_short(p, k)

    def arrive(ring, k, last):
        for p in range(len(ring.pieces)):
            ring.step_long(p, k, forward=not last)
            if not last:
                ring.step_short(p, k, forward=k < far - 1)

    def ring_steps(rings, body, before_last):
        def step(k, _):
            for ring in rings:
                arrive(ring, k, False)
            for ring in rings:
                mates(ring, k, False)
            four(k, body)
            return 0
        lax.fori_loop(1, far, step, 0)
        before_last()
        for ring in rings:
            arrive(ring, far, True)
        for ring in rings:
            mates(ring, far, True)
        pair(far, body)

    for p in range(2):
        ring_a.mate_own(p)
    pair(0, mlp_rows)
    ring_steps([ring_a], mlp_rows, lambda: ring_d.start_own(0))

    def finish_mlp(i, _):
        rows = pl.ds(pl.multiple_of(i * 64, 64), 64)
        t = x2[rows] - acc0[rows]
        x2[rows] = t
        xb[me, 0, rows] = (t * inv_rms(t)).astype(BF16)
        g = dyo[rows] + rms_back(x1[rows], acc1[rows])
        dyo[rows] = g
        xb[me, 1, rows] = g.astype(BF16)
        return 0

    lax.fori_loop(0, half // 64, finish_mlp, 0)
    ring_b.start_own(0)
    ring_b.start_own(1)
    lax.fori_loop(half // 64, toks // 64, finish_mlp, 0)
    ring_b.start_own(2)
    ring_b.start_own(3)

    ring_a.drain()
    xa[me, 0] = uc[0]
    xa[me, 1] = uc[1]
    for dev in (pc.long_dev, pc.short_dev, pc.mate):
        pl.semaphore_signal(free_sem, inc=1, device_id={"tp": dev}, device_id_type=MESH)

    lane = lax.broadcasted_iota(jnp.int32, (toks, 4 * dim), 1)

    def project(d):
        w = w4[me, 0]
        stage[d] = jnp.where(lane < dim, dot_nt(xb[d, 1], w), dot_nt(xb[d, 0], w)).astype(BF16)

    for p in range(4):
        ring_b.mate_own(p)
    ring_d.mate_own(0)
    pair(0, project)

    def send_uc():
        pl.semaphore_wait(free_sem, 3)
        ring_c.start_own(0)
        ring_c.start_own(1)

    ring_steps([ring_d, ring_b], project, send_uc)

    go[...] = jnp.zeros_like(go)
    gq[...] = jnp.zeros_like(gq)
    low = lax.broadcasted_iota(jnp.int32, (n_dev * own, 2 * dim), 1) < dim
    none = jnp.zeros((n_dev * own, 2 * dim), BF16)

    def attend(s):
        rows = pl.ds(pl.multiple_of(s * own, own), own)
        block = stage[:, rows].reshape(n_dev * own, 4 * dim)
        left, right = block[:, :2 * dim], block[:, 2 * dim:]
        scores = dot_nt(jnp.where(low, none, left), right) * scale
        ex = jnp.exp(scores - jnp.max(scores, axis=-1, keepdims=True))
        prob = ex / jnp.sum(ex, axis=-1, keepdims=True)
        prob_b = prob.astype(BF16)
        d_prob = dot_nt(jnp.where(low, left, none), right)
        d_s = (prob * (d_prob - jnp.sum(d_prob * prob, axis=-1, keepdims=True)) * scale).astype(BF16)
        out_l = jnp.where(low, dot_nn(prob_b, right), dot_nn(d_s, right))
        out_r = jnp.where(low, dot_tn(prob_b, left), dot_tn(d_s, left))
        out = jnp.concatenate([out_l, out_r], axis=1).astype(BF16)
        stage[:, rows] = out.reshape(n_dev, own, 4 * dim)
        turn = out.T
        xs = xb[:, 0, rows].reshape(n_dev * own, hidden)
        cs = xb[:, 1, rows].reshape(n_dev * own, hidden)
        go[...] += dot_nn(turn[:dim], cs)
        g3 = dot_nn(turn[dim:], xs)
        gq[0] += g3[:dim]
        gq[2] += g3[dim:2 * dim]
        gq[1] += g3[2 * dim:]

    def back(g, hop):
        dev = lax.rem(me + hop, n_dev)
        rows = pl.ds(g * group * own, group * own)
        return pltpu.make_async_remote_copy(
            src_ref=stage.at[dev, rows], dst_ref=packed.at[me, rows],
            send_sem=all_send.at[g, hop - 1], recv_sem=all_recv.at[g, hop - 1],
            device_id={"tp": dev}, device_id_type=MESH)

    for g in range(4):
        lax.fori_loop(g * group, (g + 1) * group, lambda s, _: (attend(s), 0)[1], 0)
        for hop in range(1, n_dev):
            back(g, hop).start()

    gw2[...] = jnp.zeros_like(gw2)
    accw[...] = jnp.zeros_like(accw)
    w2v = pltpu.make_async_copy(w2, uc.at[0], load_sem.at[4])
    w2v.start()
    w2v.wait()

    def mlp_cols(d):
        ud, cd = xa[d, 0], xa[d, 1]
        h, da = activation(dot_nt(ud, w1t[...]), dot_nt(cd, uc[0]))
        gw2[...] += dot_tn(h, cd)
        accw[...] += dot_tn(da, ud)

    for p in range(2):
        ring_c.mate_own(p)
    pair(0, mlp_cols)

    def finish():
        packed[me] = stage[me]
        acc0[...] = jnp.zeros_like(acc0)
        acc1[...] = jnp.zeros_like(acc1)
        for hop in range(1, n_dev):
            src = lax.rem(me + n_dev - hop, n_dev)
            for g in range(4):
                rows = pl.ds(g * group * own, group * own)
                pltpu.make_async_remote_copy(
                    src_ref=stage.at[src, rows], dst_ref=packed.at[src, rows],
                    send_sem=all_send.at[g, hop - 1], recv_sem=all_recv.at[g, hop - 1],
                    device_id={"tp": src}, device_id_type=MESH).wait_recv()

        def head(n, _):
            pk = packed[n]
            w = w4[n, 0]
            zero = jnp.zeros_like(pk)
            acc0[...] += dot_nn(jnp.where(lane < dim, pk, zero), w)
            acc1[...] += dot_nn(jnp.where(lane < dim, zero, pk), w)
            return 0

        lax.fori_loop(0, n_dev, head, 0)

        def rows_out(i, _):
            rows = pl.ds(pl.multiple_of(i * 64, 64), 64)
            x1[rows] = x1[rows] - acc0[rows]
            dx2[rows] = dx2[rows] + rms_back(x2[rows], acc1[rows])
            return 0

        lax.fori_loop(0, toks // 64, rows_out, 0)

    ring_steps([ring_c], mlp_cols, finish)
    gw1[...] = accw[...].T
    ring_b.drain()
    ring_c.drain()
    ring_d.drain()
    for g in range(4):
        for hop in range(1, n_dev):
            back(g, hop).wait_send()


def layer_backward(n_dev, y_one, y_two, dy_one, dy_two, wq, wo, wu, wd):
    seqs, own, hidden = y_one.shape
    n_loc, dim = wo.shape[0], wo.shape[1]
    toks = seqs * own
    cols = wu.shape[1]
    flat = lambda t: t.reshape(toks, hidden)
    any_spec = pl.BlockSpec(memory_space=pl.ANY)
    vmem = pl.BlockSpec(memory_space=pltpu.VMEM)
    far = n_dev // 4

    def ring_sems(p):
        dma = pltpu.SemaphoreType.DMA
        return (dma((p, far)), dma((p, far)), dma((p, far - 1)), dma((p, far - 1)), dma((p, 2 * far)), dma((p, 2 * far)))

    body = functools.partial(kernel, n_dev, seqs, own, dim, dim ** -0.5)

    def flat_body(*refs):
        main, sems = refs[:16 + 11], refs[16 + 11:]
        rings = [sems[6 * i:6 * i + 6] for i in range(4)]
        body(*main, *rings, *sems[24:])

    sems = [s for p in (2, 4, 2, 1) for s in ring_sems(p)]
    dma = pltpu.SemaphoreType.DMA
    outs = pl.pallas_call(
        flat_body,
        name="reversible_block",
        out_shape=[jax.ShapeDtypeStruct((toks, hidden), F32)] * 4 + [
            jax.ShapeDtypeStruct((3, dim, hidden), F32), jax.ShapeDtypeStruct((dim, hidden), F32),
            jax.ShapeDtypeStruct((hidden, cols), F32), jax.ShapeDtypeStruct((cols, hidden), F32)],
        in_specs=[any_spec] * 8,
        out_specs=[vmem] * 8,
        scratch_shapes=[
            pltpu.VMEM((n_dev, 2, toks, hidden), BF16),
            pltpu.VMEM((n_dev, 2, toks, hidden), BF16),
            pltpu.VMEM((n_dev, 1, 4 * dim, hidden), BF16),
            pltpu.VMEM((n_dev, toks, 4 * dim), BF16),
            pltpu.VMEM((n_dev, toks, 4 * dim), BF16),
            pltpu.VMEM((2, toks, hidden), BF16),
            pltpu.VMEM((cols, hidden), BF16),
            pltpu.VMEM((hidden, cols), BF16),
            pltpu.VMEM((toks, hidden), F32),
            pltpu.VMEM((toks, hidden), F32),
            pltpu.VMEM((cols, hidden), F32),
            *sems,
            dma((10,)),
            dma((4, n_dev - 1)),
            dma((4, n_dev - 1)),
            pltpu.SemaphoreType.REGULAR,
        ],
        compiler_params=pltpu.CompilerParams(collective_id=0, has_side_effects=True, vmem_limit_bytes=67043328),
    )(flat(y_one), flat(y_two), flat(dy_one), flat(dy_two), wu, wd, wo.reshape(n_loc * dim, hidden), wq.transpose(1, 2, 3, 0).reshape(3, dim, hidden))
    x_one, x_two, dx_one, dx_two, g_q, g_o, g_up, g_down = outs
    back = lambda t: t.reshape(y_one.shape)
    return back(x_one), back(x_two), back(dx_one), back(dx_two), g_q.reshape(n_loc, 3, dim, hidden).transpose(3, 0, 1, 2), g_o.reshape(wo.shape), g_up, g_down


def local_backward(n_dev, y_one, y_two, dy_one, dy_two, w_qkv, w_out, w_up, w_down):
    grads = []
    state = (y_one, y_two, dy_one, dy_two)
    for idx in reversed(range(w_qkv.shape[0])):
        res = layer_backward(n_dev, *state, w_qkv[idx], w_out[idx], w_up[idx], w_down[idx])
        state = res[:4]
        grads.append(res[4:])
    return state + tuple(jnp.stack(g[::-1]) for g in zip(*grads))


def solution(mesh):
    state_spec = P("dp", "tp", None)
    in_specs = (state_spec, state_spec, state_spec, state_spec, P(None, None, "tp", None, None), P(None, "tp", None, None), P(None, None, "tp"), P(None, "tp", None))
    out_specs = (state_spec, state_spec, state_spec, state_spec, P("dp", None, "tp", None, None), P("dp", "tp", None, None), P("dp", None, "tp"), P("dp", "tp", None))
    return jax.shard_map(functools.partial(local_backward, mesh.shape["tp"]), mesh=mesh, in_specs=in_specs, out_specs=out_specs, check_vma=False)
```

time: 683 us -> 358 us (0.52)
  waiting for transfers between devices: 538 us -> 0 us
  Pallas kernels: 0 us -> 346 us
  matrix products: 104 us -> 0 us
  other arithmetic: 20.7 us -> 0 us
  between operations: 14.4 us -> 0.66 us
    pallas_call x0 -> x1, Pallas kernels: none -> 346 us  [layer_backward(): pl.pallas_call(flat_body, name='reversible_block', out_shape=[jax.ShapeDt...]
    reduce_scatter x4 -> x0, waiting for transfers between devices: 342 us -> none  [scatter_positions(): return lax.psum_scatter(tensor, 'tp', scatter_dimension=1, tiled=True)]
    all_gather x4 -> x0, waiting for transfers between devices: 196 us -> none  [gather_positions(): return lax.all_gather(tensor, 'tp', axis=1, tiled=True)]
    dot_general x18 -> x0, matrix products: 104 us -> none  [the longest x1 10 us: local_backward(): jnp.einsum('bsh,fh->bsf', cot_mlp, wd_layer, preferred_element_type=jnp.f...]
    convert_element_type x4 -> x0, other arithmetic: 7.91 us -> none  [the longest x1 3.99 us: local_backward(): cot_att = gather_positions(dy_one.astype(jnp.bfloat16))]
  transfers between devices with their start and end apart: 8 -> 0, of which waited for: 8 -> 0; matrix products, arithmetic and copies ran while one was open for 9% -> 0% of each run, Pallas kernels for 0% -> 0%
where the time goes in v2:
time: 358 us
  Pallas kernels  346 us (97%)
  local copies, waits for them, and re-layouts  11.5 us (3%)
    pallas_call x1, Pallas kernels, layer_backward(): pl.pallas_call(flat_body, name='reversible_block', out_shape=[jax.ShapeDt...  346 us
    unnamed x22, local copies, waits for them, and re-layouts  11.5 us

profile of v2, /device:TPU:21, one launch (start us, length us, event | category | flops | bytes accessed | tf_op | source)
XLA Modules:
  0.0 357.9 jit_solution(11746842161431331060)
XLA Ops:
  0.6 345.8 %reversible_block.1 = (f32[256,1024]{1,0:T(8,128)}, f32[256,1024]{1,0:T(8,128)}, f32[256,1024]{1,0:T(8,128)}, f32[256,1024]{1,0:T(8,128)}, f32[3,64,1024]{2,1,0:...) custom-call(f32[256,1024]{1,0:T(8,128)} %bitcast.30, f32[256,1024]{1,0:T(8,128)} %bitcast.31, ...), custom_call_target="tpu_custom_call" | custom-call | tf_op jit(solution)/shard_map/reversible_block/pallas_call | solution.py:399
  346.4 0.0 copy-start.4
  346.4 2.4 copy.24
  348.8 0.0 copy-done.4
  348.8 0.0 copy-start.3
  348.8 1.0 copy.25
  349.8 0.6 copy-done.3
  350.4 0.0 copy-start.2
  350.4 1.0 copy.26
  351.4 0.6 copy-done.2
  352.0 0.0 copy-start.5
  352.0 1.0 copy.27
  353.0 0.5 copy-done.5
  353.5 0.0 copy-start.6
  353.5 0.0 copy-start.1
  353.5 0.9 copy.28
  354.4 0.2 copy-done.6
  354.6 0.7 copy.29
  355.3 0.0 copy-done.1
  355.3 0.0 copy-start
  355.3 1.0 copy.30
  356.3 0.6 copy-done
  356.9 1.0 copy.31
Async XLA Ops:
  346.4 2.4 copy-start.4
  348.8 1.6 copy-start.3
  350.4 1.6 copy-start.2
  352.0 1.5 copy-start.5
  353.5 1.1 copy-start.6
  353.5 1.8 copy-start.1
  355.3 1.6 copy-start
